TPU v7x, 256 devices: a whole 4x4x8 slice. The times are simulated.
256 devices in a mesh: group: 32 (over z, y_hi, core), mp: 8 (over x, y_lo).
Axes of the slice: x: 4, y: 4 (y_hi: 2, y_lo: 2; y = y_hi * 2 + y_lo), z: 8, core: 2. Of those that a mesh axis runs over, the one named last changes fastest.
Arguments:
- anchor: float32 [16, 2048, 2048], P(None, 'group', 'mp'), may hold values from -6 to 6
- momentum: float32 [16, 2048, 2048], P(None, 'group', 'mp'), may hold values from -3 to 3
- deltas: float32 [32, 2, 2048, 2048], P('group', None, None, 'mp'), may hold values from -3 to 3
- old_path: int32 [32, 2], replicated, may hold values from 0 to 7, as said below
- new_path: int32 [32, 2], replicated, may hold values from 0 to 7, as said below
- tokens: bfloat16 [32, 1024, 2048], P('group', None, 'mp'), may hold values from -40 to 40
- cotangent: bfloat16 [32, 1024, 2048], P('group', None, 'mp'), may hold values from -6 to 6
Outputs:
- new_anchor: float32 [16, 2048, 2048], P(None, 'group', 'mp')
- new_momentum: float32 [16, 2048, 2048], P(None, 'group', 'mp')
- grads: bfloat16 [32, 2, 2048, 2048], P('group', None, None, 'mp')
Inputs may be any that keep to these rules, and one draw needn't show every extreme that they name: `old_path`: for each of the 2 levels, every one of the 8 modules is named by at least one group. `new_path`: for each of the 2 levels, every one of the 8 modules is named by at least one group.
All inputs are finite; a program needn't handle non-finite values.
Results may differ from a plain program's by a relative error of at most 0.014.
Values may be sent and summed in bfloat16 or wider, within the bound.
A program may use at most 128 MiB of HBM per device.

v0:
```python
import math
import jax
import jax.numpy as jnp
from jax import lax
from jax.sharding import Mesh
from jax.sharding import PartitionSpec as P

D = 2048
MODS = 8
MP = ("mp_0", "mp_1")
outer_rate = 0.7
momentum_rate = 0.9
epsilon = 1e-06


def whole_of(x, axes, dim):
    for axis in reversed(axes):
        x = lax.all_gather(x, axis, axis=dim, tiled=True)
    return x


def cut_along(x, dim, length):
    before, after = (x.shape[:dim], x.shape[dim + 1 :])
    return jnp.moveaxis(x.reshape(*before, length, -1, *after), dim, 0)


def summed_on_arrival(x, axis, dim):
    length = lax.axis_size(axis)
    pieces = lax.all_to_all(cut_along(x, dim, length), axis, 0, 0, tiled=True)
    return jnp.sum(pieces.astype(jnp.float32), axis=0)


def silu_slope(values):
    sigmoid_part = jax.nn.sigmoid(values)
    return sigmoid_part * (1.0 + values * (1.0 - sigmoid_part))


def normalize(hidden):
    whole = whole_of(hidden, MP, 1)
    values = whole.astype(jnp.float32)
    scale = lax.rsqrt(jnp.mean(values * values, axis=-1) + epsilon)
    normed = (values * scale[:, None]).astype(jnp.bfloat16)
    return (normed, scale)


def outer_update(received, anchor_rows, momentum_rows, old_columns, new_columns):
    groups_count = received.shape[0]
    levels_count = received.shape[1]
    module_count = anchor_rows.shape[0]
    offsets = jnp.arange(levels_count, dtype=jnp.int32) * MODS
    old_index = (old_columns + offsets[None, :]).reshape(-1)
    selector = (old_index[None, :] == jnp.arange(module_count, dtype=jnp.int32)[:, None]).astype(
        jnp.float32
    )
    sums = jnp.dot(
        selector, received.reshape(groups_count * levels_count, -1), precision=lax.Precision.HIGHEST
    )
    counts = jnp.sum(selector, axis=1)
    outer_grad = (sums / counts[:, None]).reshape(anchor_rows.shape)
    new_momentum = momentum_rate * momentum_rows + outer_grad
    new_anchor = anchor_rows - outer_rate * (outer_grad + momentum_rate * new_momentum)
    new_index = new_columns + offsets[None, :]
    outgoing = jnp.take(new_anchor, new_index, axis=0).astype(jnp.bfloat16)
    return (new_anchor, new_momentum, outgoing)


def shards(anchor, momentum, deltas, old_path, new_path, tokens, cotangent):
    factor = 1.0 / math.sqrt(D)
    first_state = tokens[0]
    upstream = cotangent[0].astype(jnp.float32)
    first_normed, first_scale = normalize(first_state)
    received = lax.all_to_all(
        deltas.astype(jnp.bfloat16), "group", split_axis=2, concat_axis=0, tiled=True
    ).astype(deltas.dtype)
    new_anchor, new_momentum, outgoing = outer_update(
        received, anchor, momentum, old_path, new_path
    )
    loaded = lax.all_to_all(outgoing, "group", split_axis=0, concat_axis=2, tiled=True)
    weight_parts = [loaded[0, 0], loaded[0, 1]]
    first_weight = weight_parts[0]
    second_weight = weight_parts[1]
    first_pre = jnp.dot(first_normed, first_weight, preferred_element_type=jnp.float32) * factor
    second_state = (first_state.astype(jnp.float32) + jax.nn.silu(first_pre)).astype(jnp.bfloat16)
    second_normed, second_scale = normalize(second_state)
    second_pre = jnp.dot(second_normed, second_weight, preferred_element_type=jnp.float32) * factor
    second_slope = (upstream * silu_slope(second_pre)).astype(jnp.bfloat16)
    second_grad = (
        lax.dot_general(
            second_normed,
            second_slope,
            (((0,), (0,)), ((), ())),
            preferred_element_type=jnp.float32,
        )
        * factor
    ).astype(jnp.bfloat16)
    terms = (
        lax.dot_general(
            second_slope,
            second_weight,
            (((1,), (1,)), ((), ())),
            preferred_element_type=jnp.float32,
        )
        * factor
    )
    normed_grad = summed_on_arrival(terms.astype(jnp.bfloat16), MP, 1)
    middle = second_state.astype(jnp.float32)
    inner = lax.psum(jnp.sum(normed_grad * middle, axis=-1), MP)
    state_grad = (
        upstream
        + second_scale[:, None] * normed_grad
        - middle * (second_scale**3 * inner / D)[:, None]
    )
    first_slope = (state_grad * silu_slope(first_pre)).astype(jnp.bfloat16)
    first_grad = (
        lax.dot_general(
            first_normed, first_slope, (((0,), (0,)), ((), ())), preferred_element_type=jnp.float32
        )
        * factor
    ).astype(jnp.bfloat16)
    grads = jnp.stack([first_grad, second_grad])[None]
    return (new_anchor, new_momentum, grads)


def solution(mesh):
    split = Mesh(mesh.devices.reshape(mesh.shape["group"], 4, 2), ("group", "mp_0", "mp_1"))
    placed = (
        P(None, "group", MP),
        P(None, "group", MP),
        P("group", None, None, MP),
        P(),
        P(),
        P("group", None, MP),
        P("group", None, MP),
    )
    return jax.shard_map(
        shards,
        mesh=split,
        in_specs=placed,
        out_specs=(P(None, "group", MP), P(None, "group", MP), P("group", None, None, MP)),
        check_vma=False,
    )
```

profile of v0, /device:TPU:16, one launch (start us, length us, event | category | flops | bytes accessed | tf_op | source)
XLA Modules:
  0.0 331.8 jit_solution(7924139874974365925)
XLA Ops:
  7.2 8.6 %copy.63 = bf16[1,2,2048,256]{3,1,0,2:T(2,128)(2,1)} copy(f32[1,2,2048,256]{3,2,1,0:T(8,128)} %param.9) | data formatting | bytes 6291456 | tf_op args[2]
  15.7 11.7 %all-to-all-start = ((bf16[1,2,2048,256]{3,1,0,2:T(2,128)(2,1)}), bf16[1,2,2048,256]{3,1,0,2:T(2,128)(2,1)S(1)}, u32[]{:S(2)}, u32[]{:S(2)}) async-start(bf16[1,2,2048,256]{3,1,0,2:T(2,128)(2,1)} %copy.63), calls=%async_computation | async-start | bytes 4194304 | tf_op jit(solution)/shard_map/all_to_all | solution.py:72
  27.5 0.7 all-gather.11.cloned.1.call-update
  28.2 36.0 %all-gather.11.cloned.1.call-done = bf16[1,1024,512]{2,1,0:T(8,128)(2,1)} async-done(((bf16[1,1024,256]{2,1,0:T(8,128)(2,1)}), bf16[1,1024,512]{2,1,0:T(8,128)(2,1)}) %all-gather.11.cloned.1.call-update) | async-done | bytes 1048592 | tf_op jit(solution)/shard_map/all_gather | solution.py:18
  64.3 0.1 compare_and_fusion
  64.4 0.1 copy.48
  64.5 0.1 broadcast_add_fusion
  64.6 0.1 copy.43
  64.7 0.1 eq.15
  64.8 0.1 copy.49
  64.8 0.1 reshape.46
  65.0 0.1 convert_reduce_fusion.1
  65.1 12.5 %all-to-all-done = bf16[1,2,2048,256]{3,1,0,2:T(2,128)(2,1)S(1)} async-done(((bf16[1,2,2048,256]{3,1,0,2:T(2,128)(2,1)}), bf16[1,2,2048,256]{3,1,0,2:T(2,128)(2,1)S(1)}, u32[]{:S(2)}, u32[]{:S(2)}) %all-to-all-start) | async-done | bytes 2097184 | tf_op jit(solution)/shard_map/all_to_all | solution.py:72
  77.6 0.4 copy.45
  78.1 1.3 copy.59
  79.4 0.4 convolution_divide_fusion
  79.8 0.3 copy.60
  80.1 0.5 copy-done.7
  80.6 0.4 copy-done.8
  81.0 1.3 fusion.34
  82.4 0.8 gather_fusion
  83.1 1.7 select_convert_fusion
  84.9 6.4 %all-to-all-start.1 = ((bf16[32,2,64,256]{3,2,1,0:T(8,128)(2,1)}), bf16[32,2,64,256]{3,2,1,0:T(8,128)(2,1)S(1)}, u32[]{:S(2)}, u32[]{:S(2)}) async-start(bf16[32,2,64,256]{3,2,1,0:T(8,128)(2,1)} %select_convert_fusion), calls=%async_computation.1 | async-start | bytes 4194304 | tf_op jit(solution)/shard_map/all_to_all | solution.py:78
  91.3 0.2 copy.47
  91.5 28.5 %all-gather.13.cloned.1.call-done = bf16[1,1024,2048]{2,1,0:T(8,128)(2,1)} async-done(((bf16[1,1024,512]{2,1,0:T(8,128)(2,1)}), bf16[1,1024,2048]{2,1,0:T(8,128)(2,1)}) %all-gather.13.cloned.1.call-update) | async-done | bytes 4194320 | tf_op jit(solution)/shard_map/all_gather | solution.py:18
  120.0 3.1 fusion.2
  123.1 18.3 %all-to-all-done.1 = bf16[32,2,64,256]{3,2,1,0:T(8,128)(2,1)S(1)} async-done(((bf16[32,2,64,256]{3,2,1,0:T(8,128)(2,1)}), bf16[32,2,64,256]{3,2,1,0:T(8,128)(2,1)S(1)}, u32[]{:S(2)}, u32[]{:S(2)}) %all-to-all-start.1) | async-done | bytes 2097184 | tf_op jit(solution)/shard_map/all_to_all | solution.py:78
  141.4 0.1 copy.50
  141.6 2.8 copy-done.1
  144.4 2.8 fusion.35
  147.2 0.2 all-gather.9.cloned.1.call-start
  147.5 23.5 %all-gather.7.cloned.1.call-done = bf16[1024,512]{0,1:T(8,128)(2,1)} async-done(((bf16[1024,256]{0,1:T(8,128)(2,1)}), bf16[1024,512]{0,1:T(8,128)(2,1)}) %all-gather.7.cloned.1.call-update) | async-done | bytes 1048592 | tf_op jit(solution)/shard_map/all_gather | solution.py:18
  171.0 0.2 copy.46
  171.2 53.5 %all-gather.9.cloned.1.call-done = bf16[1024,2048]{0,1:T(8,128)(2,1)} async-done(((bf16[1024,512]{0,1:T(8,128)(2,1)}), bf16[1024,2048]{0,1:T(8,128)(2,1)}) %all-gather.9.cloned.1.call-update) | async-done | bytes 4194320 | tf_op jit(solution)/shard_map/all_gather | solution.py:18
  224.6 3.3 fusion
  227.9 0.2 copy-done.2
  228.1 1.3 fusion.25
  229.4 1.6 multiply_convert_fusion
  231.1 2.2 copy.64
  233.3 4.7 %all-to-all-start.2 = ((bf16[8,1024,256]{2,1,0:T(8,128)(2,1)}), bf16[8,1024,256]{2,1,0:T(8,128)(2,1)}, u32[]{:S(2)}, u32[]{:S(2)}) async-start(bf16[8,1024,256]{2,1,0:T(8,128)(2,1)} %bitcast.70), calls=%async_computation.2 | async-start | bytes 8388608 | tf_op jit(solution)/shard_map/all_to_all | solution.py:29
  238.0 4.6 %fusion.15 = bf16[1,2048,256]{2,1,0:T(8,128)(2,1)} fusion(bf16[1024,2048]{0,1:T(8,128)(2,1)} %all-gather.9.cloned.1.call-done, f32[1024]{0:T(1024)S(1)} %add_rsqrt_fusion, f32[1024,256]{0,1:T(8,128)S(1)} %copy-done.14, bf16[1,1024,256]{1,2,0:T(8,128)(2,1)S(1)} %copy.46), kind=kOutput, calls=%fused_computation.21 | convolution fusion | flops 1083703296 | bytes 6819840 | tf_op jit(solution)/shard_map/dot_general | solution.py:88
  242.7 55.0 %all-to-all-done.2 = bf16[8,1024,256]{2,1,0:T(8,128)(2,1)} async-done(((bf16[8,1024,256]{2,1,0:T(8,128)(2,1)}), bf16[8,1024,256]{2,1,0:T(8,128)(2,1)}, u32[]{:S(2)}, u32[]{:S(2)}) %all-to-all-start.2) | async-done | bytes 4194336 | tf_op jit(solution)/shard_map/all_to_all | solution.py:29
  297.7 2.9 convert_reduce_fusion
  300.5 0.3 copy.54
  300.9 0.2 fusion.28
  301.0 18.3 %psum.7 = f32[1024]{0:T(1024)S(1)} all-reduce(f32[1024]{0:T(1024)S(1)} %fusion.28), channel_id=1, replica_groups=mesh['group'=32,'mp_0'=4,'mp_1'=2] {'mp_0','mp_1'}, use_global_device_ids=true, to_apply=%region_5.6 | all-reduce | flops 1024 | bytes 8192 | tf_op jit(solution)/shard_map/psum | solution.py:107
  319.3 4.5 %fusion.18 = bf16[1,2048,256]{2,1,0:T(8,128)(2,1)S(1)} fusion(bf16[1,1024,2048]{2,1,0:T(8,128)(2,1)} %all-gather.13.cloned.1.call-done, f32[1024]{0:T(1024)S(1)} %add_rsqrt_fusion.1, bf16[1024,256]{0,1:T(8,128)(2,1)S(1)} %copy-done.3, f32[1024,256]{0,1:T(8,128)} %get-tuple-element.8, f32[1024,256]{0,1:T(8,128)S(1)} %copy.54, ...), kind=kOutput, calls=%fused_computation.22 | convolution fusion | flops 1085014016 | bytes 8400896 | tf_op jit(solution)/shard_map/dot_general | solution.py:115
  323.8 1.5 maximum_bitcast_fusion
  (37 shorter events, 0.3 us)
Async XLA Ops:
  15.7 48.6 %copy-start.11 = (s32[32,2]{0,1:T(2,128)S(1)}, s32[32,2]{0,1:T(2,128)}, u32[]{:S(2)}) copy-start(s32[32,2]{0,1:T(2,128)} %param.11) | copy-start | bytes 772
  15.7 48.8 %copy-start.12 = (s32[32,2]{0,1:T(2,128)S(1)}, s32[32,2]{0,1:T(2,128)}, u32[]{:S(2)}) copy-start(s32[32,2]{0,1:T(2,128)} %param.10) | copy-start | bytes 772
  15.7 61.9 %all-to-all-start = ((bf16[1,2,2048,256]{3,1,0,2:T(2,128)(2,1)}), bf16[1,2,2048,256]{3,1,0,2:T(2,128)(2,1)S(1)}, u32[]{:S(2)}, u32[]{:S(2)}) async-start(bf16[1,2,2048,256]{3,1,0,2:T(2,128)(2,1)} %copy.63), calls=%async_computation | async-start | bytes 4194304 | tf_op jit(solution)/shard_map/all_to_all | solution.py:72
  27.5 36.8 %all-gather.11.cloned.1.call-start = ((), (), s32[]{:S(2)}) async-start(), calls=%async_computation.5 | async-start | bytes 1572864 | tf_op jit(solution)/shard_map/all_gather | solution.py:18
  28.2 91.8 %all-gather.13.cloned.1.call-start = ((), (), s32[]{:S(2)}) async-start(), calls=%async_computation.6 | async-start | bytes 5242880 | tf_op jit(solution)/shard_map/all_gather | solution.py:18
  79.3 1.3 copy-start.7
  79.4 1.7 copy-start.8
  82.4 2.5 copy-start
  84.9 6.4 %copy-start.6 = (bf16[1,1024,256]{2,1,0:T(8,128)(2,1)S(1)}, bf16[1,1024,256]{2,1,0:T(8,128)(2,1)}, u32[]{:S(2)}) copy-start(bf16[1,1024,256]{2,1,0:T(8,128)(2,1)} %param.12) | copy-start | bytes 1572868
  84.9 56.6 %all-to-all-start.1 = ((bf16[32,2,64,256]{3,2,1,0:T(8,128)(2,1)}), bf16[32,2,64,256]{3,2,1,0:T(8,128)(2,1)S(1)}, u32[]{:S(2)}, u32[]{:S(2)}) async-start(bf16[32,2,64,256]{3,2,1,0:T(8,128)(2,1)} %select_convert_fusion), calls=%async_computation.1 | async-start | bytes 4194304 | tf_op jit(solution)/shard_map/all_to_all | solution.py:78
  91.3 79.7 %all-gather.7.cloned.1.call-start = ((), (), s32[]{:S(2)}) async-start(), calls=%async_computation.3 | async-start | bytes 1572864 | tf_op jit(solution)/shard_map/all_gather | solution.py:18
  141.4 2.9 copy-start.1
  141.6 5.6 %copy-start.4 = (bf16[1,2,32,64,256]{4,3,2,1,0:T(8,128)(2,1)}, bf16[1,2,32,64,256]{4,3,2,1,0:T(8,128)(2,1)S(1)}, u32[]{:S(2)}) copy-start(bf16[1,2,32,64,256]{4,3,2,1,0:T(8,128)(2,1)S(1)} %copy.50) | copy-start | bytes 6291460
  144.4 26.6 %copy-start.10 = (bf16[1,1024,256]{2,1,0:T(8,128)(2,1)S(1)}, bf16[1,1024,256]{2,1,0:T(8,128)(2,1)}, u32[]{:S(2)}) copy-start(bf16[1,1024,256]{2,1,0:T(8,128)(2,1)} %param.13) | copy-start | bytes 1572868
  147.2 80.7 %copy-start.5 = (bf16[1,2,32,64,256]{4,3,2,1,0:T(8,128)(2,1)S(1)}, bf16[1,2,32,64,256]{4,3,2,1,0:T(8,128)(2,1)}, u32[]{:S(2)}) copy-start(bf16[1,2,32,64,256]{4,3,2,1,0:T(8,128)(2,1)} %copy-done.4) | copy-start | bytes 6291460
  147.2 77.4 %all-gather.9.cloned.1.call-start = ((), (), s32[]{:S(2)}) async-start(), calls=%async_computation.4 | async-start | bytes 5242880 | tf_op jit(solution)/shard_map/all_gather | solution.py:18
  224.6 3.4 %copy-start.2 = (bf16[1024,2048]{0,1:T(8,128)(2,1)S(1)}, bf16[1024,2048]{0,1:T(8,128)(2,1)}, u32[]{:S(2)}) copy-start(bf16[1024,2048]{0,1:T(8,128)(2,1)} %all-gather.9.cloned.1.call-done) | copy-start | bytes 12582916
  229.4 1.7 copy-start.13
  233.3 4.7 %copy-start.14 = (f32[1024,256]{0,1:T(8,128)S(1)}, f32[1024,256]{0,1:T(8,128)}, u32[]{:S(2)}) copy-start(f32[1024,256]{0,1:T(8,128)} %copy-done.13) | copy-start | bytes 3145732
  233.3 64.4 %all-to-all-start.2 = ((bf16[8,1024,256]{2,1,0:T(8,128)(2,1)}), bf16[8,1024,256]{2,1,0:T(8,128)(2,1)}, u32[]{:S(2)}, u32[]{:S(2)}) async-start(bf16[8,1024,256]{2,1,0:T(8,128)(2,1)} %bitcast.70), calls=%async_computation.2 | async-start | bytes 8388608 | tf_op jit(solution)/shard_map/all_to_all | solution.py:29
  242.7 58.2 %copy-start.3 = (bf16[1024,256]{0,1:T(8,128)(2,1)S(1)}, bf16[1024,256]{0,1:T(8,128)(2,1)}, u32[]{:S(2)}) copy-start(bf16[1024,256]{0,1:T(8,128)(2,1)} %get-tuple-element.7) | copy-start | bytes 1572868
  319.3 4.5 %copy-start.9 = (bf16[1,2048,256]{2,1,0:T(8,128)(2,1)S(1)}, bf16[1,2048,256]{2,1,0:T(8,128)(2,1)}, u32[]{:S(2)}) copy-start(bf16[1,2048,256]{2,1,0:T(8,128)(2,1)} %fusion.15) | copy-start | bytes 3145732
Sparse Core Ops, SparseCore 0:
  30.1 34.1 all-gather.10
  66.1 53.8 all-gather.12
  147.4 23.5 all-gather.6
  172.6 52.0 all-gather.8
where the time goes:
time: 332 us
  waiting for transfers between devices  228 us (69%)
  starting transfers between devices  23.2 us (7%)
  local copies, waits for them, and re-layouts  18.9 us (6%)
  blocking collectives  18.3 us (6%)
  matrix products  15.3 us (5%)
  other arithmetic  14.2 us (4%)
  between operations  14 us (4%)
    all_gather x4, waiting for transfers between devices, whole_of(): x = lax.all_gather(x, axis, axis=dim, tiled=True)  141 us
    all_to_all x1, waiting for transfers between devices, summed_on_arrival(): pieces = lax.all_to_all(cut_along(x, dim, length), axis, 0, 0, tiled=True)  55 us
    all_to_all x1, waiting for transfers between devices, shards(): lax.all_to_all(outgoing, 'group', split_axis=0, concat_axis=2, tiled=True)  18.3 us
    psum x1, blocking collectives, shards(): inner = lax.psum(jnp.sum(normed_grad * middle, axis=-1), MP)  18.3 us
    unnamed x35, local copies, waits for them, and re-layouts  14.5 us
    all_to_all x1, waiting for transfers between devices, shards(): lax.all_to_all(deltas.astype(jnp.bfloat16), 'group', split_axis=2, concat...  12.5 us
    all_to_all x1, starting transfers between devices, shards(): lax.all_to_all(deltas.astype(jnp.bfloat16), 'group', split_axis=2, concat...  11.7 us
  transfers between devices with their start and end apart: 7, of which 7 were waited for; matrix products, arithmetic and copies ran while one was open for 5% of the time, Pallas kernels for 0%

commit v1 on v0

--- a/solution.py
+++ b/solution.py
@@ -75,7 +75,12 @@
     new_anchor, new_momentum, outgoing = outer_update(
         received, anchor, momentum, old_path, new_path
     )
-    loaded = lax.all_to_all(outgoing, "group", split_axis=0, concat_axis=2, tiled=True)
+    loaded = jnp.concatenate(
+        lax.all_to_all(
+            jnp.stack(jnp.split(outgoing, lax.axis_size("group"), axis=0)), "group", 0, 0
+        ),
+        axis=2,
+    )
     weight_parts = [loaded[0, 0], loaded[0, 1]]
     first_weight = weight_parts[0]
     second_weight = weight_parts[1]

time: 332 us -> 353 us (1.063)
  local copies, waits for them, and re-layouts: 18.9 us -> 40.5 us
    unnamed x35 -> x66, local copies, waits for them, and re-layouts: 14.5 us -> 35.5 us
    all_gather x4, waiting for transfers between devices: 141 us -> 121 us  [whole_of(): x = lax.all_gather(x, axis, axis=dim, tiled=True)]
    all_to_all x1, waiting for transfers between devices: 18.3 us -> 37.9 us  [shards(): lax.all_to_all(jnp.stack(jnp.split(outgoing, lax.axis_size('group'), axis...]
  transfers between devices with their start and end apart: 7 -> 7, of which waited for: 7 -> 7; matrix products, arithmetic and copies ran while one was open for 5% -> 10% of each run, Pallas kernels for 0% -> 0%
where the time goes in v1:
time: 353 us; the launch traced here: 352 us
  waiting for transfers between devices  228 us (65%)
  local copies, waits for them, and re-layouts  40.5 us (11%)
  starting transfers between devices  23.1 us (7%)
  blocking collectives  18.3 us (5%)
  matrix products  15.3 us (4%)
  between operations  14 us (4%)
  other arithmetic  12.9 us (4%)
    all_gather x4, waiting for transfers between devices, whole_of(): x = lax.all_gather(x, axis, axis=dim, tiled=True)  121 us
    all_to_all x1, waiting for transfers between devices, summed_on_arrival(): pieces = lax.all_to_all(cut_along(x, dim, length), axis, 0, 0, tiled=True)  55 us
    all_to_all x1, waiting for transfers between devices, shards(): lax.all_to_all(jnp.stack(jnp.split(outgoing, lax.axis_size('group'), axis...  37.9 us
    unnamed x66, local copies, waits for them, and re-layouts  35.5 us
    psum x1, blocking collectives, shards(): inner = lax.psum(jnp.sum(normed_grad * middle, axis=-1), MP)  18.3 us
    all_to_all x1, waiting for transfers between devices, shards(): lax.all_to_all(deltas.astype(jnp.bfloat16), 'group', split_axis=2, concat...  13.3 us
    all_to_all x1, starting transfers between devices, shards(): lax.all_to_all(deltas.astype(jnp.bfloat16), 'group', split_axis=2, concat...  11.7 us
  transfers between devices with their start and end apart: 7, of which 7 were waited for; matrix products, arithmetic and copies ran while one was open for 10% of the time, Pallas kernels for 0%

profile of v1, /device:TPU:16, one launch (start us, length us, event | category | flops | bytes accessed | tf_op | source)
XLA Modules:
  0.0 352.1 jit_solution(1747499497317735349)
XLA Ops:
  7.2 8.6 %copy.87 = bf16[1,2,2048,256]{3,1,0,2:T(2,128)(2,1)} copy(f32[1,2,2048,256]{3,2,1,0:T(8,128)} %param.9) | data formatting | bytes 6291456 | tf_op args[2]
  15.7 11.7 %all-to-all-start = ((bf16[1,2,2048,256]{3,1,0,2:T(2,128)(2,1)}), bf16[1,2,2048,256]{3,1,0,2:T(2,128)(2,1)S(1)}, u32[]{:S(2)}, u32[]{:S(2)}) async-start(bf16[1,2,2048,256]{3,1,0,2:T(2,128)(2,1)} %copy.87), calls=%async_computation | async-start | bytes 4194304 | tf_op jit(solution)/shard_map/all_to_all | solution.py:72
  27.5 0.7 all-gather.11.cloned.1.call-update
  29.1 35.2 %all-gather.11.cloned.1.call-done = bf16[1,1024,512]{2,1,0:T(8,128)(2,1)} async-done(((bf16[1,1024,256]{2,1,0:T(8,128)(2,1)}), bf16[1,1024,512]{2,1,0:T(8,128)(2,1)}) %all-gather.11.cloned.1.call-update) | async-done | bytes 1048592 | tf_op jit(solution)/shard_map/all_gather | solution.py:18
  64.3 13.3 %all-to-all-done = bf16[1,2,2048,256]{3,1,0,2:T(2,128)(2,1)S(1)} async-done(((bf16[1,2,2048,256]{3,1,0,2:T(2,128)(2,1)}), bf16[1,2,2048,256]{3,1,0,2:T(2,128)(2,1)S(1)}, u32[]{:S(2)}, u32[]{:S(2)}) %all-to-all-start) | async-done | bytes 2097184 | tf_op jit(solution)/shard_map/all_to_all | solution.py:72
  78.1 1.3 copy.83
  80.1 1.0 copy-done.7
  81.5 1.3 fusion.34
  82.8 0.8 gather_fusion
  84.2 0.6 fusion.78
  84.8 0.6 fusion.77
  85.5 0.6 fusion.76
  86.1 0.6 fusion.75
  86.7 0.6 fusion.74
  87.4 0.6 fusion.73
  88.0 0.6 fusion.72
  88.6 0.6 fusion.71
  89.3 0.6 fusion.70
  89.9 0.6 fusion.69
  90.5 0.6 fusion.68
  91.2 0.6 fusion.67
  91.8 0.6 fusion.66
  92.4 0.6 fusion.65
  93.1 0.6 fusion.64
  93.7 0.6 fusion.63
  94.3 0.6 fusion.62
  102.6 0.6 fusion.49
  103.8 0.6 fusion.47
  104.5 6.3 %all-to-all-start.1 = ((bf16[32,1,2,64,256]{4,3,2,1,0:T(8,128)(2,1)}), bf16[32,1,2,64,256]{4,3,2,1,0:T(8,128)(2,1)S(1)}, u32[]{:S(2)}, u32[]{:S(2)}) async-start(bf16[32,1,2,64,256]{4,3,2,1,0:T(8,128)(2,1)} %fusion.47), calls=%async_computation.1 | async-start | bytes 4194304 | tf_op jit(solution)/shard_map/all_to_all | solution.py:79
  111.1 8.9 %all-gather.13.cloned.1.call-done = bf16[1,1024,2048]{2,1,0:T(8,128)(2,1)} async-done(((bf16[1,1024,512]{2,1,0:T(8,128)(2,1)}), bf16[1,1024,2048]{2,1,0:T(8,128)(2,1)}) %all-gather.13.cloned.1.call-update) | async-done | bytes 4194320 | tf_op jit(solution)/shard_map/all_gather | solution.py:18
  120.0 3.1 fusion.2
  123.1 37.9 %all-to-all-done.1 = bf16[32,1,2,64,256]{4,3,2,1,0:T(8,128)(2,1)S(1)} async-done(((bf16[32,1,2,64,256]{4,3,2,1,0:T(8,128)(2,1)}), bf16[32,1,2,64,256]{4,3,2,1,0:T(8,128)(2,1)S(1)}, u32[]{:S(2)}, u32[]{:S(2)}) %all-to-all-start.1) | async-done | bytes 2097184 | tf_op jit(solution)/shard_map/all_to_all | solution.py:79
  161.1 2.8 copy-done.1
  163.9 2.8 fusion.35
  167.0 23.5 %all-gather.7.cloned.1.call-done = bf16[1024,512]{0,1:T(8,128)(2,1)} async-done(((bf16[1024,256]{0,1:T(8,128)(2,1)}), bf16[1024,512]{0,1:T(8,128)(2,1)}) %all-gather.7.cloned.1.call-update) | async-done | bytes 1048592 | tf_op jit(solution)/shard_map/all_gather | solution.py:18
  190.7 53.5 %all-gather.9.cloned.1.call-done = bf16[1024,2048]{0,1:T(8,128)(2,1)} async-done(((bf16[1024,512]{0,1:T(8,128)(2,1)}), bf16[1024,2048]{0,1:T(8,128)(2,1)}) %all-gather.9.cloned.1.call-update) | async-done | bytes 4194320 | tf_op jit(solution)/shard_map/all_gather | solution.py:18
  244.2 3.3 fusion
  247.7 1.3 fusion.25
  249.0 1.6 multiply_convert_fusion
  250.7 2.2 copy.88
  252.9 4.7 %all-to-all-start.2 = ((bf16[8,1024,256]{2,1,0:T(8,128)(2,1)}), bf16[8,1024,256]{2,1,0:T(8,128)(2,1)}, u32[]{:S(2)}, u32[]{:S(2)}) async-start(bf16[8,1024,256]{2,1,0:T(8,128)(2,1)} %bitcast.197), calls=%async_computation.2 | async-start | bytes 8388608 | tf_op jit(solution)/shard_map/all_to_all | solution.py:29
  257.6 4.6 %fusion.15 = bf16[1,2048,256]{2,1,0:T(8,128)(2,1)} fusion(bf16[1024,2048]{0,1:T(8,128)(2,1)} %all-gather.9.cloned.1.call-done, f32[1024]{0:T(1024)S(1)} %add_rsqrt_fusion, f32[1024,256]{0,1:T(8,128)S(1)} %copy-done.14, bf16[1,1024,256]{1,2,0:T(8,128)(2,1)S(1)} %copy.70), kind=kOutput, calls=%fused_computation.21 | convolution fusion | flops 1083703296 | bytes 6819840 | tf_op jit(solution)/shard_map/dot_general | solution.py:93
  262.2 55.0 %all-to-all-done.2 = bf16[8,1024,256]{2,1,0:T(8,128)(2,1)} async-done(((bf16[8,1024,256]{2,1,0:T(8,128)(2,1)}), bf16[8,1024,256]{2,1,0:T(8,128)(2,1)}, u32[]{:S(2)}, u32[]{:S(2)}) %all-to-all-start.2) | async-done | bytes 4194336 | tf_op jit(solution)/shard_map/all_to_all | solution.py:29
  317.2 2.9 convert_reduce_fusion
  320.5 0.7 copy-done.3
  321.3 18.3 %psum.7 = f32[1024]{0:T(1024)S(1)} all-reduce(f32[1024]{0:T(1024)S(1)} %fusion.28), channel_id=1, replica_groups=mesh['group'=32,'mp_0'=4,'mp_1'=2] {'mp_0','mp_1'}, use_global_device_ids=true, to_apply=%region_5.6 | all-reduce | flops 1024 | bytes 8192 | tf_op jit(solution)/shard_map/psum | solution.py:112
  339.6 4.5 %fusion.18 = bf16[1,2048,256]{2,1,0:T(8,128)(2,1)S(1)} fusion(bf16[1,1024,2048]{2,1,0:T(8,128)(2,1)} %all-gather.13.cloned.1.call-done, f32[1024]{0:T(1024)S(1)} %add_rsqrt_fusion.1, bf16[1024,256]{0,1:T(8,128)(2,1)S(1)} %copy-done.3, f32[1024,256]{0,1:T(8,128)} %get-tuple-element.8, f32[1024,256]{0,1:T(8,128)S(1)} %copy.78, ...), kind=kOutput, calls=%fused_computation.22 | convolution fusion | flops 1085014016 | bytes 8400896 | tf_op jit(solution)/shard_map/dot_general | solution.py:120
  344.1 1.5 maximum_bitcast_fusion
  (69 shorter events, 12.8 us)
Async XLA Ops:
  15.7 12.5 %copy-start.11 = (s32[32,2]{0,1:T(2,128)S(1)}, s32[32,2]{0,1:T(2,128)}, u32[]{:S(2)}) copy-start(s32[32,2]{0,1:T(2,128)} %param.11) | copy-start | bytes 772
  15.7 12.7 %copy-start.12 = (s32[32,2]{0,1:T(2,128)S(1)}, s32[32,2]{0,1:T(2,128)}, u32[]{:S(2)}) copy-start(s32[32,2]{0,1:T(2,128)} %param.10) | copy-start | bytes 772
  15.7 61.9 %all-to-all-start = ((bf16[1,2,2048,256]{3,1,0,2:T(2,128)(2,1)}), bf16[1,2,2048,256]{3,1,0,2:T(2,128)(2,1)S(1)}, u32[]{:S(2)}, u32[]{:S(2)}) async-start(bf16[1,2,2048,256]{3,1,0,2:T(2,128)(2,1)} %copy.87), calls=%async_computation | async-start | bytes 4194304 | tf_op jit(solution)/shard_map/all_to_all | solution.py:72
  27.5 36.8 %all-gather.11.cloned.1.call-start = ((), (), s32[]{:S(2)}) async-start(), calls=%async_computation.5 | async-start | bytes 1572864 | tf_op jit(solution)/shard_map/all_gather | solution.py:18
  28.2 91.8 %all-gather.13.cloned.1.call-start = ((), (), s32[]{:S(2)}) async-start(), calls=%async_computation.6 | async-start | bytes 5242880 | tf_op jit(solution)/shard_map/all_gather | solution.py:18
  79.7 1.3 copy-start.7
  79.8 1.7 copy-start.8
  82.8 1.0 copy-start
  104.5 6.4 %copy-start.6 = (bf16[1,1024,256]{2,1,0:T(8,128)(2,1)S(1)}, bf16[1,1024,256]{2,1,0:T(8,128)(2,1)}, u32[]{:S(2)}) copy-start(bf16[1,1024,256]{2,1,0:T(8,128)(2,1)} %param.12) | copy-start | bytes 1572868
  104.5 56.5 %all-to-all-start.1 = ((bf16[32,1,2,64,256]{4,3,2,1,0:T(8,128)(2,1)}), bf16[32,1,2,64,256]{4,3,2,1,0:T(8,128)(2,1)S(1)}, u32[]{:S(2)}, u32[]{:S(2)}) async-start(bf16[32,1,2,64,256]{4,3,2,1,0:T(8,128)(2,1)} %fusion.47), calls=%async_computation.1 | async-start | bytes 4194304 | tf_op jit(solution)/shard_map/all_to_all | solution.py:79
  110.8 79.7 %all-gather.7.cloned.1.call-start = ((), (), s32[]{:S(2)}) async-start(), calls=%async_computation.3 | async-start | bytes 1572864 | tf_op jit(solution)/shard_map/all_gather | solution.py:18
  161.0 2.9 copy-start.1
  161.1 5.6 %copy-start.4 = (bf16[32,1,2,64,256]{4,3,0,2,1:T(8,128)(2,1)}, bf16[32,1,2,64,256]{4,3,0,2,1:T(8,128)(2,1)S(1)}, u32[]{:S(2)}) copy-start(bf16[32,1,2,64,256]{4,3,0,2,1:T(8,128)(2,1)S(1)} %copy.74) | copy-start | bytes 6291460
  163.9 26.6 %copy-start.10 = (bf16[1,1024,256]{2,1,0:T(8,128)(2,1)S(1)}, bf16[1,1024,256]{2,1,0:T(8,128)(2,1)}, u32[]{:S(2)}) copy-start(bf16[1,1024,256]{2,1,0:T(8,128)(2,1)} %param.13) | copy-start | bytes 1572868
  166.8 77.4 %all-gather.9.cloned.1.call-start = ((), (), s32[]{:S(2)}) async-start(), calls=%async_computation.4 | async-start | bytes 5242880 | tf_op jit(solution)/shard_map/all_gather | solution.py:18
  190.5 57.0 %copy-start.5 = (bf16[32,1,2,64,256]{4,3,0,2,1:T(8,128)(2,1)S(1)}, bf16[32,1,2,64,256]{4,3,0,2,1:T(8,128)(2,1)}, u32[]{:S(2)}) copy-start(bf16[32,1,2,64,256]{4,3,0,2,1:T(8,128)(2,1)} %copy-done.4) | copy-start | bytes 6291460
  244.2 3.4 copy-start.2
  249.0 1.7 copy-start.13
  252.9 4.7 %copy-start.14 = (f32[1024,256]{0,1:T(8,128)S(1)}, f32[1024,256]{0,1:T(8,128)}, u32[]{:S(2)}) copy-start(f32[1024,256]{0,1:T(8,128)} %copy-done.13) | copy-start | bytes 3145732
  252.9 64.4 %all-to-all-start.2 = ((bf16[8,1024,256]{2,1,0:T(8,128)(2,1)}), bf16[8,1024,256]{2,1,0:T(8,128)(2,1)}, u32[]{:S(2)}, u32[]{:S(2)}) async-start(bf16[8,1024,256]{2,1,0:T(8,128)(2,1)} %bitcast.197), calls=%async_computation.2 | async-start | bytes 8388608 | tf_op jit(solution)/shard_map/all_to_all | solution.py:29
  320.1 1.0 copy-start.3
  339.6 4.5 %copy-start.9 = (bf16[1,2048,256]{2,1,0:T(8,128)(2,1)S(1)}, bf16[1,2048,256]{2,1,0:T(8,128)(2,1)}, u32[]{:S(2)}) copy-start(bf16[1,2048,256]{2,1,0:T(8,128)(2,1)} %fusion.15) | copy-start | bytes 3145732
Sparse Core Ops, SparseCore 0:
  30.1 34.1 all-gather.10
  66.1 53.8 all-gather.12
  166.9 23.5 all-gather.6
  192.2 52.0 all-gather.8
